TPU v7x, 32 devices: a whole 2x2x4 slice. The times are simulated.
32 devices in a mesh: freq: 8 (over y, x, core), base: 4 (over z).
Axes of the slice: x: 2, y: 2, z: 4, core: 2. Of those that a mesh axis runs over, the one named last changes fastest.
Arguments:
- visibility: float32 [2, 16, 2048], P(None, 'freq', 'base'), may hold values from -6 to 6
- tile_of: int32 [16, 2048, 1], P('freq', 'base'), may hold values from 0 to 3; in each aligned block of 512 rows (0 to 511, 512 to 1023, ..., all dimensions but the last counted through in order) at most 256 rows name the same one
- u_within: int32 [16, 2048], P('freq', 'base'), may hold values from 0 to 255
- v_cell: int32 [16, 2048], P('freq', 'base'), may hold values from 0 to 1016
- kernel_index: int32 [2, 16, 2048], P(None, 'freq', 'base'), may hold values from 0 to 127
- kernel: float32 [128, 8], replicated, may hold values from 0.1 to 1
- live_count: int32 [16, 4], P('freq', 'base'), may hold values from 64 to 512, as said below
- bin_map: int32 [1024, 1024], P('base'), may hold values from 0 to 511, as said below
Outputs:
- power_map: float32 [1024, 1024], P('freq', 'base')
- spectrum: float32 [512], replicated
Inputs may be any that keep to these rules, and one draw needn't show every extreme that they name: `tile_of`: among the visibilities of one channel on one device, at most 256 name the same tile, and in some device's visibilities a tile is named by exactly 256. `live_count`: the first device along base holds 512 used slots in every channel; the used slots of a device are its first ones. `bin_map`: every bin number occurs.
All inputs are finite; a program needn't handle non-finite values.
Results may differ from a plain program's by a relative error of at most 0.0003.
Values sent between devices are 32-bit elements; how exact they have to be, the bound alone decides.
A program may use at most 128 MiB of HBM per device.

v0:
```python
import math

import jax
import jax.numpy as jnp
from jax import lax
from jax.sharding import PartitionSpec as P

G = 1024
NBINS = 512
KW = 8


HIGHEST_PRECISION = lax.Precision.HIGHEST


def passed_along(x, axis, by):
    peers = lax.axis_size(axis)
    pairs = [(i, i + by) for i in range(peers) if 0 <= i + by < peers]
    return lax.ppermute(x, axis, pairs)


def look_up_taps(kernel_index, kernel):
    table_rows = kernel.shape[0]
    onehot = (kernel_index[..., None] == jnp.arange(table_rows, dtype=jnp.int32)).astype(
        jnp.float32
    )
    return jnp.einsum("acno,ot->actn", onehot, kernel, precision=HIGHEST_PRECISION)


def visibility_fields(
    visibility, tile_of, u_within, v_cell, kernel_index, kernel, live_count, tile_rows
):
    slots = u_within.shape[1]
    is_live = jnp.arange(slots, dtype=jnp.int32)[None, :] < live_count
    zeroed = jnp.zeros_like(visibility[0])
    real_part = jnp.where(is_live, visibility[0], zeroed)
    imag_part = jnp.where(is_live, visibility[1], zeroed)
    tile_index = tile_of[:, :, 0]
    u_cell = jnp.minimum(tile_index * tile_rows + u_within, G - KW)
    u_cell = u_cell - tile_index * tile_rows
    taps = look_up_taps(kernel_index, kernel)
    fields = jnp.concatenate(
        [
            real_part[:, None],
            imag_part[:, None],
            u_cell[:, None].astype(jnp.float32),
            v_cell[:, None].astype(jnp.float32),
            taps[0],
            taps[1],
        ],
        axis=1,
    )
    return (fields, is_live, tile_index)


def row_taps(fields, row_start, row_count):
    u_cell = fields[2].astype(jnp.int32)
    offset = row_start + jnp.arange(row_count, dtype=jnp.int32)[None, :] - u_cell[:, None]
    taps = jnp.zeros(offset.shape, jnp.float32)
    for tap_index in range(KW):
        taps = taps + jnp.where(offset == tap_index, fields[4 + tap_index][:, None], 0.0)
    return taps


def column_side(fields):
    v_start = fields[3].astype(jnp.int32)
    offset = jnp.arange(G, dtype=jnp.int32)[None, :] - v_start[:, None]
    taps = jnp.zeros(offset.shape, jnp.float32)
    for tap_index in range(KW):
        taps = taps + jnp.where(offset == tap_index, fields[4 + KW + tap_index][:, None], 0.0)
    return jnp.concatenate([fields[0][:, None] * taps, fields[1][:, None] * taps], axis=1)


def contract_slots(upper, lower):
    return lax.dot_general(upper, lower, (((0,), (0,)), ((), ())), precision=HIGHEST_PRECISION)


def grid_rows(fields, row_start, row_count):
    return contract_slots(row_taps(fields, row_start, row_count), column_side(fields))


def dft_matrix():
    positions = jnp.arange(G, dtype=jnp.int32)
    phase = positions[:, None] * positions[None, :] % G
    angle = phase.astype(jnp.float32) * (2.0 * math.pi / G)
    cosine = jnp.cos(angle)
    sine = jnp.sin(angle)
    return jnp.concatenate(
        [jnp.concatenate([cosine, -sine], axis=1), jnp.concatenate([sine, cosine], axis=1)], axis=0
    )


def row_transform(grid_tile, dft_table, tile_rows, channels_here):
    flat_rows = grid_tile.reshape(tile_rows * channels_here, 2 * G)
    halves = jnp.stack(
        [
            jnp.dot(flat_rows, dft_table[:, :G], precision=HIGHEST_PRECISION),
            jnp.dot(flat_rows, dft_table[:, G:], precision=HIGHEST_PRECISION),
        ]
    )
    return halves.reshape(2, tile_rows, channels_here, G)


def to_columns(columns, tile_rows, channels_here):
    return columns.reshape(2 * G, channels_here * tile_rows)


def histogram(stacked, bins):
    row_total = bins.shape[0]
    block_rows = min(64, row_total)
    block_count = row_total // block_rows
    columns = bins.shape[1]
    value_blocks = stacked.reshape(2, block_count, block_rows * columns).transpose(1, 0, 2)
    bin_blocks = bins.reshape(block_count, block_rows * columns)

    def add_block(running, pieces):
        values, bin_ids = pieces
        onehot = (bin_ids[:, None] == jnp.arange(NBINS, dtype=jnp.int32)[None, :]).astype(
            jnp.float32
        )
        return (running + jnp.dot(values, onehot, precision=HIGHEST_PRECISION), None)

    result, _ = lax.scan(add_block, jnp.zeros((2, NBINS), jnp.float32), (value_blocks, bin_blocks))
    return result


def per_device(visibility, tile_of, u_within, v_cell, kernel_index, kernel, live_count, bin_map):
    base_count = lax.axis_size("base")
    freq_count = lax.axis_size("freq")
    tile_rows = G // base_count
    channels_here = visibility.shape[1]
    slots = visibility.shape[2]
    dft_table = dft_matrix()
    fields, is_live, tile_index = visibility_fields(
        visibility, tile_of, u_within, v_cell, kernel_index, kernel, live_count, tile_rows
    )
    capacity = 2 * slots // base_count
    field_count = fields.shape[1]
    chosen = (
        (tile_index[:, :, None] == jnp.arange(base_count, dtype=jnp.int32)[None, None, :])
        & is_live[:, :, None]
    ).astype(jnp.int32)
    before_count = jnp.sum((jnp.cumsum(chosen, axis=1) - chosen) * chosen, axis=2)
    target = jnp.where(is_live, tile_index * capacity + before_count, base_count * capacity)
    outgoing = []
    for channel in range(channels_here):
        placed = (
            jnp.zeros((base_count * capacity, field_count), jnp.float32)
            .at[target[channel]]
            .set(fields[channel].T, mode="drop")
        )
        outgoing.append(placed.reshape(base_count, capacity, field_count).transpose(0, 2, 1))
    received = lax.all_to_all(
        jnp.stack(outgoing, axis=1), "base", split_axis=0, concat_axis=0, tiled=True
    )
    extended = []
    for channel in range(channels_here):
        slot_fields = (
            received[:, channel].transpose(1, 0, 2).reshape(field_count, base_count * capacity)
        )
        extended.append(grid_rows(slot_fields, 0, tile_rows + KW).reshape(tile_rows + KW, 2, G))
    extended = jnp.stack(extended, axis=1)
    incoming = passed_along(extended[tile_rows:], "base", 1)
    grid_tile = extended[:tile_rows].at[:KW].add(incoming)
    halves = row_transform(grid_tile, dft_table, tile_rows, channels_here)
    columns = lax.all_to_all(halves, "base", split_axis=3, concat_axis=1, tiled=True)
    stacked = to_columns(columns, tile_rows, channels_here)
    spectra = contract_slots(dft_table, stacked)
    normalizer = 1.0 / (channels_here * freq_count * slots * base_count)
    squared = spectra[:G] * spectra[:G] + spectra[G:] * spectra[G:]
    power_part = jnp.sum(squared.reshape(G, channels_here, tile_rows), axis=1) * normalizer
    bins_here = bin_map.T
    share_rows = G // freq_count
    share_start = lax.axis_index("freq") * share_rows
    power_share = lax.psum_scatter(power_part, "freq", scatter_dimension=0, tiled=True)
    bins_share = lax.dynamic_slice_in_dim(bins_here, share_start, share_rows, 0)
    bin_sums_local = histogram(jnp.stack([power_share, jnp.ones_like(power_share)]), bins_share)
    totals, counts = lax.psum((bin_sums_local[0], bin_sums_local[1]), ("freq", "base"))
    return (power_share, totals / counts)


def solution(mesh):
    in_specs = (
        P(None, "freq", "base"),
        P("freq", "base", None),
        P("freq", "base"),
        P("freq", "base"),
        P(None, "freq", "base"),
        P(),
        P("freq", "base"),
        P("base", None),
    )
    out_specs = (P("freq", "base"), P())
    return jax.shard_map(
        per_device, mesh=mesh, in_specs=in_specs, out_specs=out_specs, check_vma=False
    )
```

profile of v0, /device:TPU:0, one launch (start us, length us, event | category | flops | bytes accessed | tf_op | source)
XLA Modules:
  0.0 432.0 jit_solution(2849988539622279299)
XLA Ops:
  10.1 2.4 reduce-window.6
  14.8 1.6 convolution_bitcast_fusion
  18.3 1.8 scatter_custom_fusion
  20.5 1.8 scatter_custom_fusion.1
  23.4 6.3 %all-to-all-start = ((f32[4,2,20,256]{3,1,2,0:T(2,128)}), f32[4,2,20,256]{3,1,2,0:T(2,128)S(1)}, u32[]{:S(2)}, u32[]{:S(2)}) async-start(f32[4,2,20,256]{3,1,2,0:T(2,128)} %copy.65), calls=%async_computation | async-start | bytes 327680 | tf_op jit(solution)/shard_map/all_to_all | solution.py:153
  29.7 17.5 %fusion.36 = (f32[1024,1024]{1,0:T(8,128)}, f32[1024,1024]{1,0:T(8,128)}) fusion(), kind=kLoop, calls=%fused_computation.59 | loop fusion | flops 14680064 | bytes 8388608 | tf_op jit(solution)/shard_map/sin | solution.py:87
  47.3 16.5 %fusion.38 = f32[1024,1024]{1,0:T(8,128)} fusion(), kind=kLoop, calls=%fused_computation.61 | loop fusion | flops 15728640 | bytes 4194304 | tf_op jit(solution)/shard_map/neg | solution.py:89
  64.2 4.4 %broadcast_multiply_fusion.1 = (f32[1024,1024]{1,0:T(8,128)S(1)}, f32[1024,1024]{1,0:T(8,128)S(1)}) fusion(f32[1024]{0:T(1024)S(1)} %bitcast.240, f32[1024]{0:T(1024)S(1)} %bitcast.258, f32[1024]{0:T(1024)S(1)} %bitcast.256, f32[1024]{0:T(1024)S(1)} %bitcast.254, f32[1024]{0:T(1024)S(1)} %bitcast.252, f32[1024]{0:T(1024)S(1)} %bitcast.250, ...), kind=kLoop, calls=%fused_computation.56 | loop fusion | flops 27262976 | bytes 8433664 | tf_op jit(solution)/shard_map/mul | solution.py:71
  68.6 10.1 %fusion.9 = f32[264,2048]{1,0:T(8,128)} fusion(f32[1024,1024]{1,0:T(8,128)S(1)} %get-tuple-element.127, f32[1024,1024]{1,0:T(8,128)S(1)} %get-tuple-element.126, f32[1024]{0:T(1024)S(1)} %bitcast.276, f32[1024]{0:T(1024)S(1)} %bitcast.274, f32[1024]{0:T(1024)S(1)} %bitcast.272, f32[1024]{0:T(1024)S(1)} %bitcast.270, f32[1024]{0:T(1024)S(1)} %bitcast.284, ...), kind=kOutput, calls=%fused_computation.18 | convolution fusion | flops 6652362752 | bytes 10588160 | tf_op jit(solution)/shard_map/dot_general | solution.py:75
  78.7 3.2 stack_reshape.7
  82.1 4.1 broadcast_multiply_fusion.3
  86.2 10.1 %fusion.5 = f32[264,2048]{1,0:T(8,128)} fusion(f32[1024,1024]{1,0:T(8,128)S(1)} %get-tuple-element.129, f32[1024,1024]{1,0:T(8,128)S(1)} %get-tuple-element.128, f32[1024]{0:T(1024)S(1)} %bitcast.285, f32[1024]{0:T(1024)S(1)} %bitcast.283, f32[1024]{0:T(1024)S(1)} %bitcast.281, f32[1024]{0:T(1024)S(1)} %bitcast.279, f32[1024]{0:T(1024)S(1)} %bitcast.277, ...), kind=kOutput, calls=%fused_computation.14 | convolution fusion | flops 6652362752 | bytes 10588160 | tf_op jit(solution)/shard_map/dot_general | solution.py:75
  96.3 4.1 stack_reshape.6
  100.4 2.5 constant_dynamic-update-slice_fusion.1
  103.8 3.9 collective-permute-start
  107.8 12.9 %maximum_maximum_fusion = f32[2048,2048]{1,0:T(8,128)} fusion(f32[1024,1024]{1,0:T(8,128)S(1)} %copy-done.3, f32[1024,1024]{1,0:T(8,128)S(1)} %copy-done.1, f32[1024,1024]{1,0:T(8,128)} %fusion.38), kind=kLoop, calls=%fused_computation.9 | loop fusion | flops 12582912 | bytes 29360128 | tf_op jit(solution)/shard_map/concatenate | solution.py:88
  120.7 3.4 slice.363
  124.8 6.7 %reshape.405 = f32[256,2,2048]{2,0,1:T(8,128)} reshape(f32[256,2,2,1024]{3,2,0,1:T(2,128)} %fusion.144) | data formatting | bytes 8388608 | tf_op jit(solution)/shard_map/reshape.292
  131.5 16.9 %fusion.39 = f32[1,256,2,1024]{3,1,2,0:T(8,128)S(1)} fusion(f32[256,2,2048]{2,0,1:T(8,128)} %reshape.405, f32[2048,2048]{1,0:T(8,128)} %maximum_maximum_fusion), kind=kOutput, calls=%fused_computation.62 | convolution fusion | flops 12884901888 | bytes 14680064 | tf_op jit(solution)/shard_map/dot_general | solution.py:97
  148.4 16.3 %fusion.40 = f32[1,256,2,1024]{3,1,2,0:T(8,128)S(1)} fusion(f32[256,2,2048]{2,0,1:T(8,128)S(1)} %copy-done.5, f32[2048,2048]{1,0:T(8,128)} %maximum_maximum_fusion), kind=kOutput, calls=%fused_computation.63 | convolution fusion | flops 12884901888 | bytes 14680064 | tf_op jit(solution)/shard_map/dot_general | solution.py:98
  164.7 2.3 pad_maximum_fusion
  167.0 7.2 %copy.68 = f32[2,256,2,1024]{1,2,0,3:T(2,128)} copy(f32[2,256,2,1024]{3,1,2,0:T(8,128)} %pad_maximum_fusion) | data formatting | bytes 8388608 | tf_op jit(solution)/shard_map/stack | solution.py:95
  174.2 98.3 %all_to_all.20 = f32[2,256,2,1024]{1,2,0,3:T(2,128)} all-to-all(f32[2,256,2,1024]{1,2,0,3:T(2,128)} %copy.68), channel_id=1, replica_groups=mesh['freq'=8,'base'=4] {'base'}, dimensions={3} | all-to-all | bytes 8388608 | tf_op jit(solution)/shard_map/all_to_all | solution.py:166
  272.5 10.9 %copy.69 = f32[2,256,2,4,256]{4,2,1,3,0:T(2,128)} copy(f32[2,256,2,4,256]{1,2,0,4,3:T(2,128)} %bitcast.228) | data formatting | bytes 8388608 | tf_op jit(solution)/shard_map/all_to_all | solution.py:166
  283.4 4.9 %copy.120 = f32[256,8,2,256]{3,1,2,0:T(8,128)} copy(f32[256,8,2,256]{3,2,1,0:T(2,128)} %bitcast.229) | data formatting | bytes 8388608
  289.6 33.1 %fusion.175 = f32[2048,512]{0,1:T(8,128)S(1)} fusion(f32[2048,512]{1,0:T(8,128)} %bitcast.231, f32[1024,1024]{1,0:T(8,128)S(1)} %copy-done.4, f32[1024,1024]{1,0:T(8,128)S(1)} %copy-done.2, f32[1024,1024]{1,0:T(8,128)} %fusion.38), kind=kOutput, calls=%fused_computation.257 | convolution fusion | flops 25782386688 | bytes 20971520 | tf_op jit(solution)/shard_map/dot_general | solution.py:75
  324.4 2.3 broadcast_multiply_fusion.4
  327.0 34.9 %reduce-scatter.2.cloned.1.call-done = f32[128,256]{0,1:T(8,128)} async-done(((f32[1024,256]{0,1:T(8,128)}), f32[128,256]{0,1:T(8,128)}) %reduce-scatter.2.cloned.1.call-update) | async-done | bytes 131088 | tf_op jit(solution)/shard_map/reduce_scatter | solution.py:175
  363.1 21.1 %while.12 = (s32[]{:T(128)}, f32[2,512]{1,0:T(2,128)S(1)}, f32[2,2,16384]{2,0,1:T(2,128)S(1)}, s32[2,16384]{1,0:T(2,128)S(1)}, s32[]{:T(128)}, /*index=5*/s32[]{:T(128)}) while((s32[]{:T(128)}, f32[2,512]{1,0:T(2,128)S(1)}, f32[2,2,16384]{2,0,1:T(2,128)S(1)}, s32[2,16384]{1,0:T(2,128)S(1)}, s32[]{:T(128)}, ...), condition=%wide.region_8.9_spmd.clone, body=%wide.region_7.8_spmd.clone.sunk | while | flops 209717248 | bytes 598103 | solution.py:123
  363.4 10.3 %fusion.183 = f32[2,512]{1,0:T(2,128)S(1)} fusion(s32[16384]{0:T(1024)S(1)} %bitcast.235, f32[1,2,16384]{2,0,1:T(1,128)S(1)} %constant_dynamic-slice_fusion.5, f32[2,512]{1,0:T(2,128)S(1)} %get-tuple-element.176, pred[]{:T(512)S(6)} %compare.11), kind=kOutput, calls=%fused_computation.5.clone.1 | convolution fusion | flops 209717248 | bytes 204801 | tf_op jit(solution)/shard_map/while/body/eval_jaxpr/dot_general | solution.py:121
  373.9 10.3 %fusion.183 = f32[2,512]{1,0:T(2,128)S(1)} fusion(s32[16384]{0:T(1024)S(1)} %bitcast.235, f32[1,2,16384]{2,0,1:T(1,128)S(1)} %constant_dynamic-slice_fusion.5, f32[2,512]{1,0:T(2,128)S(1)} %get-tuple-element.176, pred[]{:T(512)S(6)} %compare.11), kind=kOutput, calls=%fused_computation.5.clone.1 | convolution fusion | flops 209717248 | bytes 204801 | tf_op jit(solution)/shard_map/while/body/eval_jaxpr/dot_general | solution.py:121
  384.2 39.3 %all-reduce.1 = (f32[512]{0:T(512)S(1)}, f32[512]{0:T(512)S(1)}) all-reduce(f32[512]{0:T(512)S(1)} %bitcast.265, f32[512]{0:T(512)S(1)} %bitcast.264), channel_id=1, replica_groups=mesh['freq'=8,'base'=4] {'freq','base'}, use_global_device_ids=true, to_apply=%region_9.10 | all-reduce | flops 1024 | bytes 8192 | tf_op jit(solution)/shard_map/psum | solution.py:178
  (109 shorter events, 16.5 us)
Async XLA Ops:
  7.2 319.6 %copy-start = (s32[256,1024]{1,0:T(8,128)S(1)}, s32[256,1024]{1,0:T(8,128)}, u32[]{:S(2)}) copy-start(s32[256,1024]{1,0:T(8,128)} %param.19) | copy-start | bytes 3145732
  23.4 40.4 %all-to-all-start = ((f32[4,2,20,256]{3,1,2,0:T(2,128)}), f32[4,2,20,256]{3,1,2,0:T(2,128)S(1)}, u32[]{:S(2)}, u32[]{:S(2)}) async-start(f32[4,2,20,256]{3,1,2,0:T(2,128)} %copy.65), calls=%async_computation | async-start | bytes 327680 | tf_op jit(solution)/shard_map/all_to_all | solution.py:153
  29.7 332.2 %reduce-scatter.2.cloned.1.call-start = ((), (), s32[]{:S(2)}) async-start(), calls=%async_computation.3 | async-start | bytes 1179648 | tf_op jit(solution)/shard_map/reduce_scatter | solution.py:175
  100.4 7.4 %copy-start.1 = (f32[1024,1024]{1,0:T(8,128)S(1)}, f32[1024,1024]{1,0:T(8,128)}, u32[]{:S(2)}) copy-start(f32[1024,1024]{1,0:T(8,128)} %get-tuple-element.142) | copy-start | bytes 12582916
  100.4 7.4 %copy-start.3 = (f32[1024,1024]{1,0:T(8,128)S(1)}, f32[1024,1024]{1,0:T(8,128)}, u32[]{:S(2)}) copy-start(f32[1024,1024]{1,0:T(8,128)} %get-tuple-element.143) | copy-start | bytes 12582916
  103.8 20.3 %collective-permute-start = (f32[8,2,2,1024]{3,2,0,1:T(2,128)S(1)}, f32[8,2,2,1024]{3,2,0,1:T(2,128)S(1)}, u32[]{:S(2)}, u32[]{:S(2)}) collective-permute-start(f32[8,2,2,1024]{3,2,0,1:T(2,128)S(1)} %slice.365), channel_id=1, source_target_pairs={{0,1},{1,2},{2,3},{4,5},{5,6},{6,7},{8,9},{9,10},{10,11},{12,13},{... | collective-permute-start | bytes 393224 | tf_op jit(solution)/shard_map/ppermute | solution.py:19
  131.5 16.9 %copy-start.5 = (f32[256,2,2048]{2,0,1:T(8,128)S(1)}, f32[256,2,2048]{2,0,1:T(8,128)}, u32[]{:S(2)}) copy-start(f32[256,2,2048]{2,0,1:T(8,128)} %reshape.405) | copy-start | bytes 12582916
  283.4 4.9 %copy-start.2 = (f32[1024,1024]{1,0:T(8,128)S(1)}, f32[1024,1024]{1,0:T(8,128)}, u32[]{:S(2)}) copy-start(f32[1024,1024]{1,0:T(8,128)} %get-tuple-element.142) | copy-start | bytes 12582916
  283.4 6.2 %copy-start.4 = (f32[1024,1024]{1,0:T(8,128)S(1)}, f32[1024,1024]{1,0:T(8,128)}, u32[]{:S(2)}) copy-start(f32[1024,1024]{1,0:T(8,128)} %get-tuple-element.143) | copy-start | bytes 12582916
  363.1 61.0 %copy-start.6 = (f32[128,256]{0,1:T(8,128)S(1)}, f32[128,256]{0,1:T(8,128)}, u32[]{:S(2)}) copy-start(f32[128,256]{0,1:T(8,128)} %reduce-scatter.2.cloned.1.call-done) | copy-start | bytes 393220
Sparse Core Ops, SparseCore 0:
  326.8 35.0 reduce-scatter.1
where the time goes:
time: 440 us; the launch traced here: 432 us
  blocking collectives  138 us (31%)
  matrix products  109 us (25%)
  other arithmetic  70.4 us (16%)
  local copies, waits for them, and re-layouts  55.1 us (13%)
  waiting for transfers between devices  35 us (8%)
  between operations  14.9 us (3%)
  starting transfers between devices  10.3 us (2%)
    all_to_all x1, blocking collectives, per_device(): lax.all_to_all(halves, 'base', split_axis=3, concat_axis=1, tiled=True)  98.3 us
    dot_general x3, matrix products, contract_slots(): lax.dot_general(upper, lower, (((0,), (0,)), ((), ())), precision=HIGHEST...  53.3 us
    psum x1, blocking collectives, per_device(): lax.psum((bin_sums_local[0], bin_sums_local[1]), ('freq', 'base'))  39.3 us
    reduce_scatter x1, waiting for transfers between devices, per_device(): lax.psum_scatter(power_part, 'freq', scatter_dimension=0, tiled=True)  34.9 us
    dot_general x2, matrix products, add_block(): jnp.dot(values, onehot, precision=HIGHEST_PRECISION)  20.6 us
    sin x1, other arithmetic, dft_matrix(): sine = jnp.sin(angle)  17.5 us
    dot_general x1, matrix products, row_transform(): jnp.dot(flat_rows, dft_table[:, :G], precision=HIGHEST_PRECISION)  16.9 us
    neg x1, other arithmetic, dft_matrix(): -sine  16.5 us
  transfers between devices with their start and end apart: 3, of which 1 were waited for; matrix products, arithmetic and copies ran while one was open for 12% of the time, Pallas kernels for 0%

commit v1 on v0

v1 whole, which is shorter than its diff:
```python
import functools
import math

import jax
import jax.numpy as jnp
import numpy as np
from jax import lax
from jax.experimental import pallas as pl
from jax.experimental.pallas import tpu as pltpu
from jax.sharding import PartitionSpec as P

NBINS = 512
BIN_LOW = 32
KW = 8
FINE = 32
SPREAD = FINE + KW
RADIX = 4
GROUP = 16


def halves_of(x):
    high = x.astype(jnp.bfloat16)
    low = (x - high.astype(jnp.float32)).astype(jnp.bfloat16)
    return high, low


def numpy_halves(x):
    x = np.asarray(x, np.float32)
    high = x.astype(jnp.bfloat16)
    low = (x - high.astype(np.float32)).astype(jnp.bfloat16)
    return high, low


def turn(product, grid):
    angle = (product % grid) * (2.0 * math.pi / grid)
    return np.cos(angle), np.sin(angle)


@functools.lru_cache(None)
def tables(grid, blocks):
    width = grid // blocks
    l = np.arange(grid)
    c, s = turn(np.arange(SPREAD)[:, None] * l[None, :], grid)
    c, s = (x.reshape(SPREAD, blocks, width) for x in (c, s))
    fine = np.concatenate(
        [np.concatenate([c, -s], axis=2), np.concatenate([s, c], axis=2)], axis=0
    ).transpose(1, 0, 2)
    fh, fl = numpy_halves(fine)
    pad = np.zeros((blocks, 256 - 6 * SPREAD, 2 * width), fh.dtype)
    fine = np.concatenate([fh, fl, fh, pad], axis=1)
    coarse_count = grid // FINE
    c, s = turn(np.arange(coarse_count)[:, None] * FINE * l[None, :], grid)
    c, s = (x.reshape(coarse_count, blocks, width) for x in (c, s))
    ch, cl = numpy_halves(np.concatenate([c, -s], axis=2).transpose(1, 0, 2))
    coarse = np.concatenate([ch, cl], axis=1)
    slab = grid // RADIX
    u = RADIX * np.arange(slab)[None, None, :] + np.arange(RADIX)[:, None, None]
    c, s = turn(np.arange(slab)[None, :, None] * u, grid)
    dh, dl = numpy_halves(np.concatenate([c, s], axis=1))
    return fine, coarse, dh, dl


def dot(a, b):
    return jnp.dot(a, b, preferred_element_type=jnp.float32)


def dot_slots(a, b):
    return lax.dot_general(a, b, (((0,), (0,)), ((), ())), preferred_element_type=jnp.float32)


def image_kernel(
    grid, scale, f_ref, fine_ref, coarse_ref, dh_ref, dl_ref, out_ref, q_ref, rh_ref, rl_ref,
    wh_ref, wl_ref, zh_ref, zl_ref, h_ref, y_ref
):
    channel, chunk = pl.program_id(0), pl.program_id(1)
    chunks = pl.num_programs(1)
    slots = f_ref.shape[2]
    width = out_ref.shape[1]
    slab = grid // RADIX
    period = RADIX * GROUP
    re, im = f_ref[0, 0:1, :], f_ref[0, 1:2, :]
    u = f_ref[0, 2:3, :].astype(jnp.int32)
    v = f_ref[0, 3:4, :].astype(jnp.int32)

    for first in range(RADIX):
        residue = RADIX * lax.broadcasted_iota(jnp.int32, (GROUP, slots), 0) + first
        tap = (residue - u) & (period - 1)
        group = (u + tap - residue) // period
        r = jnp.zeros((GROUP, slots), jnp.float32)
        for t in range(KW):
            r = jnp.where(tap == t, f_ref[0, 4 + t:5 + t, :], r)
        rh, rl = halves_of(r)
        q_ref[first] = group.astype(jnp.float32).astype(jnp.bfloat16)
        rh_ref[first] = rh
        rl_ref[first] = rl

    piece = min(512, slots)
    for start in range(0, slots, piece):
        at = slice(start, start + piece)
        vp = v[:, at]
        offset = lax.broadcasted_iota(jnp.int32, (SPREAD, piece), 0) - (vp & (FINE - 1))
        spread = jnp.zeros((SPREAD, piece), jnp.float32)
        for t in range(KW):
            spread = jnp.where(offset == t, f_ref[0, 4 + KW + t:5 + KW + t, at], spread)
        both = jnp.concatenate([spread * re[:, at], spread * im[:, at]], axis=0)
        bh, bl = halves_of(both)
        pad = jnp.zeros((256 - 6 * SPREAD, piece), jnp.bfloat16)
        zb = dot_slots(jnp.concatenate([bh, bh, bl, pad], axis=0), fine_ref[...])
        count = coarse_ref.shape[0]
        pick = lax.broadcasted_iota(jnp.int32, (count, piece), 0) & (count // 2 - 1)
        onehot = jnp.where(pick == vp // FINE, 1.0, 0.0).astype(jnp.bfloat16)
        e = dot_slots(onehot, coarse_ref[...])
        zr, zi = zb[:, :width], zb[:, width:]
        er, ei = e[:, :width], e[:, width:]
        z = jnp.concatenate([zr * er - zi * ei, zr * ei + zi * er], axis=1)
        zh, zl = halves_of(z)
        zh_ref[at, :] = zh
        zl_ref[at, :] = zl

    def slab_step(first, carry):
        q, rh, rl = q_ref[first], rh_ref[first], rl_ref[first]
        zero = jnp.zeros_like(rh)
        for g in range(slab // GROUP):
            hit = q == jnp.bfloat16(g)
            wh_ref[g * GROUP:(g + 1) * GROUP, :] = jnp.where(hit, rh, zero)
            wl_ref[g * GROUP:(g + 1) * GROUP, :] = jnp.where(hit, rl, zero)
        zh = zh_ref[...]
        wh = wh_ref[...]
        rows = dot(wh, zh) + dot(wh, zl_ref[...]) + dot(wl_ref[...], zh)

        @pl.when(chunk == 0)
        def _():
            h_ref[first] = rows

        @pl.when(chunk > 0)
        def _():
            h_ref[first] += rows

        return carry

    lax.fori_loop(0, RADIX, slab_step, 0)

    @pl.when((channel == 0) & (chunk == 0))
    def _():
        out_ref[...] = jnp.zeros_like(out_ref)

    @pl.when(chunk == chunks - 1)
    def _():
        def transform_step(first, carry):
            hh, hl = halves_of(h_ref[first])
            dh = dh_ref[first]
            y_ref[first] = dot(dh, hh) + dot(dh, hl) + dot(dl_ref[first], hh)
            return carry

        lax.fori_loop(0, RADIX, transform_step, 0)

        def combine(block, carry):
            rows = 32
            top = pl.multiple_of(block * rows, rows)
            low = pl.multiple_of(slab + block * rows, rows)
            yr, yi = [], []
            for first in range(RADIX):
                cy = y_ref[first, pl.ds(top, rows), :]
                sy = y_ref[first, pl.ds(low, rows), :]
                yr.append(cy[:, :width] + sy[:, width:])
                yi.append(cy[:, width:] - sy[:, :width])
            ar, ai = yr[0] + yr[2], yi[0] + yi[2]
            br, bi = yr[0] - yr[2], yi[0] - yi[2]
            cr, ci = yr[1] + yr[3], yi[1] + yi[3]
            dr, di = yr[1] - yr[3], yi[1] - yi[3]
            parts = [
                (ar + cr, ai + ci), (br + di, bi - dr), (ar - cr, ai - ci), (br - di, bi + dr)
            ]
            for k, (xr, xi) in enumerate(parts):
                at = pl.ds(pl.multiple_of(k * slab + block * rows, rows), rows)
                out_ref[at, :] += (xr * xr + xi * xi) * scale
            return carry

        lax.fori_loop(0, slab // 32, combine, 0)


def image_power(fields, fine, coarse, dh, dl, grid, scale):
    channels, field_count, total = fields.shape
    width = fine.shape[1] // 2
    chunk = min(2048, total)
    slab = grid // RADIX
    bf16, f32 = jnp.bfloat16, jnp.float32
    full = lambda x: pl.BlockSpec(x.shape, lambda c, n: (0,) * x.ndim)
    return pl.pallas_call(
        functools.partial(image_kernel, grid, scale),
        grid=(channels, total // chunk),
        out_shape=jax.ShapeDtypeStruct((grid, width), f32),
        in_specs=[
            pl.BlockSpec((1, field_count, chunk), lambda c, n: (c, 0, n)),
            full(fine), full(coarse), full(dh), full(dl),
        ],
        out_specs=pl.BlockSpec((grid, width), lambda c, n: (0, 0)),
        scratch_shapes=[
            pltpu.VMEM((RADIX, GROUP, chunk), bf16),
            pltpu.VMEM((RADIX, GROUP, chunk), bf16),
            pltpu.VMEM((RADIX, GROUP, chunk), bf16),
            pltpu.VMEM((slab, chunk), bf16),
            pltpu.VMEM((slab, chunk), bf16),
            pltpu.VMEM((chunk, 2 * width), bf16),
            pltpu.VMEM((chunk, 2 * width), bf16),
            pltpu.VMEM((RADIX, slab, 2 * width), f32),
            pltpu.VMEM((RADIX, 2 * slab, 2 * width), f32),
        ],
        compiler_params=pltpu.CompilerParams(
            vmem_limit_bytes=60 * 2**20, dimension_semantics=("arbitrary", "arbitrary")
        ),
    )(fields, fine, coarse, dh, dl)


def histogram_kernel(power_ref, bins_ref, out_ref, a_ref, b_ref):
    rows, columns = power_ref.shape
    high_count = NBINS // BIN_LOW
    bins = bins_ref[...].T
    for k in range(rows):
        at = slice(k * columns, (k + 1) * columns)
        value = power_ref[k:k + 1, :]
        bin_id = bins[k:k + 1, :]
        hit = lax.broadcasted_iota(jnp.int32, (high_count, columns), 0) == bin_id // BIN_LOW
        high = value.astype(jnp.bfloat16).astype(jnp.float32)
        low = value - high
        a_ref[0:high_count, at] = jnp.where(hit, high, 0.0).astype(jnp.bfloat16)
        a_ref[high_count:2 * high_count, at] = jnp.where(hit, low, 0.0).astype(jnp.bfloat16)
        a_ref[2 * high_count:, at] = jnp.where(hit, 1.0, 0.0).astype(jnp.bfloat16)
        hit = lax.broadcasted_iota(jnp.int32, (BIN_LOW, columns), 0) == bin_id % BIN_LOW
        b_ref[:, at] = jnp.where(hit, 1.0, 0.0).astype(jnp.bfloat16)
    sums = lax.dot_general(
        a_ref[...], b_ref[...], (((1,), (1,)), ((), ())), preferred_element_type=jnp.float32
    )
    out_ref[0] = sums[:high_count] + sums[high_count:2 * high_count]
    out_ref[1] = sums[2 * high_count:]


def histogram(power, bins):
    high_count = NBINS // BIN_LOW
    return pl.pallas_call(
        histogram_kernel,
        out_shape=jax.ShapeDtypeStruct((2, high_count, BIN_LOW), jnp.float32),
        scratch_shapes=[
            pltpu.VMEM((3 * high_count, power.size), jnp.bfloat16),
            pltpu.VMEM((BIN_LOW, power.size), jnp.bfloat16),
        ],
    )(power, bins)


def look_up_taps(kernel_index, kernel):
    rows = kernel.shape[0]
    onehot = (kernel_index[:, :, None, :] == jnp.arange(rows, dtype=jnp.int32)[:, None]).astype(
        jnp.float32
    )
    return jnp.einsum("acon,ot->actn", onehot, kernel, precision=lax.Precision.HIGHEST)


def per_device(visibility, tile_of, u_within, v_cell, kernel_index, kernel, live_count, bin_map):
    base_count = lax.axis_size("base")
    freq_count = lax.axis_size("freq")
    grid = bin_map.shape[1]
    tile_rows = grid // base_count
    channels_here, slots = u_within.shape
    fine, coarse, dh, dl = tables(grid, base_count)
    here = lax.axis_index("base")
    fine = lax.dynamic_index_in_dim(jnp.asarray(fine), here, 0, keepdims=False)
    coarse = lax.dynamic_index_in_dim(jnp.asarray(coarse), here, 0, keepdims=False)

    is_live = jnp.arange(slots, dtype=jnp.int32)[None, :] < live_count
    vis = jnp.where(is_live[None], visibility, 0.0)
    u_cell = jnp.minimum(tile_of[:, :, 0] * tile_rows + u_within, grid - KW)
    taps = look_up_taps(kernel_index, kernel)
    fields = jnp.concatenate(
        [
            vis.transpose(1, 0, 2),
            u_cell[:, None].astype(jnp.float32),
            v_cell[:, None].astype(jnp.float32),
            taps[0],
            taps[1],
            jnp.zeros((channels_here, 4, slots), jnp.float32),
        ],
        axis=1,
    )
    fields = lax.all_gather(fields, "base", axis=2, tiled=True)
    scale = 1.0 / (channels_here * freq_count * slots * base_count)
    power_part = image_power(fields, fine, coarse, jnp.asarray(dh), jnp.asarray(dl), grid, scale)
    share_rows = grid // freq_count
    power_share = lax.psum_scatter(power_part, "freq", scatter_dimension=0, tiled=True)
    bins_share = lax.dynamic_slice_in_dim(
        bin_map, lax.axis_index("freq") * share_rows, share_rows, 1
    )
    sums = lax.psum(histogram(power_share, bins_share), ("freq", "base"))
    return (power_share, (sums[0] / sums[1]).reshape(NBINS))


def solution(mesh):
    in_specs = (
        P(None, "freq", "base"),
        P("freq", "base", None),
        P("freq", "base"),
        P("freq", "base"),
        P(None, "freq", "base"),
        P(),
        P("freq", "base"),
        P("base", None),
    )
    out_specs = (P("freq", "base"), P())
    return jax.shard_map(
        per_device, mesh=mesh, in_specs=in_specs, out_specs=out_specs, check_vma=False
    )
```

time: 440 us -> 147 us (0.33); the launches traced: 432 us -> 147 us
  matrix products: 109 us -> 0.42 us
  blocking collectives: 138 us -> 56.3 us
  other arithmetic: 70.4 us -> 0.1 us
  local copies, waits for them, and re-layouts: 55.1 us -> 6.89 us
  Pallas kernels: 0 us -> 31.7 us
  starting transfers between devices: 10.3 us -> 0.04 us
    dot_general x8 -> x1, matrix products: 109 us -> 0.42 us  [look_up_taps(): jnp.einsum('acon,ot->actn', onehot, kernel, precision=lax.Precision.HIGHEST)]
    all_to_all x1 -> x0, blocking collectives: 98.3 us -> none  [per_device(): lax.all_to_all(halves, 'base', split_axis=3, concat_axis=1, tiled=True)]
    pallas_call x0 -> x2, Pallas kernels: none -> 31.7 us  [the longest x1 28.9 us: image_power(): pl.pallas_call(functools.partial(image_kernel, grid, scale), grid=(channe...]
    another operation x9 -> x0, local copies, waits for them, and re-layouts: 23.1 us -> none  [the longest x3 8.12 us: per_device(): extended = jnp.stack(extended, axis=1)]
    sin x1 -> x0, other arithmetic: 17.5 us -> none  [dft_matrix(): sine = jnp.sin(angle)]
    all_gather x0 -> x1, blocking collectives: none -> 16.8 us  [per_device(): fields = lax.all_gather(fields, 'base', axis=2, tiled=True)]
    neg x1 -> x0, other arithmetic: 16.5 us -> none  [dft_matrix(): -sine]
    concatenate x1 -> x0, other arithmetic: 12.9 us -> none  [dft_matrix(): jnp.concatenate([jnp.concatenate([cosine, -sine], axis=1), jnp.concatenat...]
  transfers between devices with their start and end apart: 3 -> 1, of which waited for: 1 -> 1; matrix products, arithmetic and copies ran while one was open for 12% -> 0% of each run, Pallas kernels for 0% -> 0%
where the time goes in v1:
time: 147 us
  blocking collectives  56.3 us (38%)
  waiting for transfers between devices  37.3 us (25%)
  Pallas kernels  31.7 us (22%)
  between operations  14.1 us (10%)
  local copies, waits for them, and re-layouts  6.89 us (5%)
    psum x1, blocking collectives, per_device(): sums = lax.psum(histogram(power_share, bins_share), ('freq', 'base'))  39.5 us
    reduce_scatter x1, waiting for transfers between devices, per_device(): lax.psum_scatter(power_part, 'freq', scatter_dimension=0, tiled=True)  37.3 us
    pallas_call x1, Pallas kernels, image_power(): pl.pallas_call(functools.partial(image_kernel, grid, scale), grid=(channe...  28.9 us
    all_gather x1, blocking collectives, per_device(): fields = lax.all_gather(fields, 'base', axis=2, tiled=True)  16.8 us
  transfers between devices with their start and end apart: 1, of which 1 were waited for; matrix products, arithmetic and copies ran while one was open for 0% of the time, Pallas kernels for 0%

profile of v1, /device:TPU:0, one launch (start us, length us, event | category | flops | bytes accessed | tf_op | source)
XLA Modules:
  0.0 146.9 jit_solution(1029445984085662931)
XLA Ops:
  7.2 0.0 copy-start
  7.2 0.0 reduce-scatter.2.cloned.1.call-start
  7.2 1.8 %dynamic-slice_bitcast_fusion.fine_ref = bf16[256,512]{1,0:T(8,128)(2,1)} fusion(bf16[4,256,512]{2,1,0:T(8,128)(2,1)} %constant.39.clone, s32[]{:T(128)S(6)} %select_n.14), kind=kLoop, calls=%fused_computation.3 | loop fusion | bytes 524292 | tf_op jit(solution)/shard_map/jit(dynamic_index_in_dim)/squeeze | solution.py:266
  9.0 0.0 copy-start.6
  9.0 0.0 copy-start.7
  9.0 1.5 %dynamic-slice_bitcast_fusion.1.coarse_ref = bf16[64,512]{1,0:T(8,128)(2,1)} fusion(bf16[4,64,512]{2,1,0:T(8,128)(2,1)} %constant.40.clone, s32[]{:T(128)S(6)} %select_n.14), kind=kLoop, calls=%fused_computation.4 | loop fusion | bytes 131076 | tf_op jit(solution)/shard_map/jit(dynamic_index_in_dim)/squeeze | solution.py:267
  10.5 0.0 copy-done.6
  10.5 0.0 copy-done.7
  10.5 0.4 convolution_bitcast_fusion
  10.9 0.0 copy-start.5
  10.9 0.0 copy-start.3
  11.0 0.0 copy-start.2
  11.0 0.6 copy-done.5
  11.6 0.1 iota_compare_fusion.2
  11.7 0.0 copy-done.3
  11.7 0.0 copy-done.2
  11.7 0.0 copy-start.4
  11.7 0.7 copy-done.4
  12.4 0.0 copy-start.1
  12.4 0.7 copy-done.1
  13.1 0.3 concatenate.3
  13.4 16.8 %all_gather.3.f_ref = f32[2,24,2048]{2,1,0:T(8,128)} all-gather(f32[2,24,512]{2,1,0:T(8,128)S(1)} %concatenate.3), channel_id=1, replica_groups=mesh['freq'=8,'base'=4] {'base'}, dimensions={2}, use_global_device_ids=true | all-gather | bytes 491520 | tf_op jit(solution)/shard_map/all_gather | solution.py:284
  30.1 28.9 %shard_map.131 = f32[1024,256]{1,0:T(8,128)} custom-call(f32[2,24,2048]{2,1,0:T(8,128)} %all_gather.3.f_ref, bf16[256,512]{1,0:T(8,128)(2,1)} %dynamic-slice_bitcast_fusion.fine_ref, bf16[64,512]{1,0:T(8,128)(2,1)} %dynamic-slice_bitcast_fusion.1.coarse_ref, bf16[4,512,256]{2,1,0:T(8,128)(2,1)} %constant.41.clone.dh_ref, ...), custom_call_target="tpu_custom_call" | custom-call | tf_op jit(solution)/shard_map/pallas_call | solution.py:189
  59.1 0.0 reduce-scatter.2.cloned.1.call-update
  59.1 0.0 copy-done
  59.1 0.7 constant_dynamic-slice_fusion.bins_ref
  59.8 37.3 %reduce-scatter.2.cloned.1.call-done.power_ref = f32[128,256]{1,0:T(8,128)} async-done(((f32[1024,256]{1,0:T(8,128)}), f32[128,256]{1,0:T(8,128)}) %reduce-scatter.2.cloned.1.call-update) | async-done | bytes 131088 | tf_op jit(solution)/shard_map/reduce_scatter | solution.py:288
  97.0 2.8 %shard_map.132 = f32[2,16,32]{2,1,0:T(8,128)} custom-call(f32[128,256]{1,0:T(8,128)} %reduce-scatter.2.cloned.1.call-done.power_ref, s32[256,128]{1,0:T(8,128)} %constant_dynamic-slice_fusion.bins_ref), custom_call_target="tpu_custom_call" | custom-call | tf_op jit(solution)/shard_map/pallas_call | solution.py:240
  99.9 39.5 %psum.7 = f32[2,16,32]{2,1,0:T(8,128)S(1)} all-reduce(f32[2,16,32]{2,1,0:T(8,128)} %shard_map.132), channel_id=1, replica_groups=mesh['freq'=8,'base'=4] {'freq','base'}, use_global_device_ids=true, to_apply=%region_1.2 | all-reduce | flops 1024 | bytes 8192 | tf_op jit(solution)/shard_map/psum | solution.py:292
  139.4 0.7 div.8
  (8 shorter events, 0.0 us)
Async XLA Ops:
  7.2 51.9 %copy-start = (s32[256,1024]{1,0:T(8,128)S(1)}, s32[256,1024]{1,0:T(8,128)}, u32[]{:S(2)}) copy-start(s32[256,1024]{1,0:T(8,128)} %param.19) | copy-start | bytes 3145732
  7.2 89.9 %reduce-scatter.2.cloned.1.call-start = ((), (), s32[]{:S(2)}) async-start(), calls=%async_computation.1 | async-start | bytes 1179648 | tf_op jit(solution)/shard_map/reduce_scatter | solution.py:288
  9.0 1.5 %copy-start.6 = (s32[2,2,512]{2,1,0:T(2,128)S(1)}, s32[2,2,512]{2,1,0:T(2,128)}, u32[]{:S(2)}) copy-start(s32[2,2,512]{2,1,0:T(2,128)} %param.16) | copy-start | bytes 24580
  9.0 1.5 %copy-start.7 = (f32[128,8]{0,1:T(8,128)S(1)}, f32[128,8]{0,1:T(8,128)}, u32[]{:S(2)}) copy-start(f32[128,8]{0,1:T(8,128)} %param.17) | copy-start | bytes 12292
  10.9 0.7 copy-start.5
  10.9 0.7 copy-start.3
  11.0 0.7 copy-start.2
  11.7 0.7 copy-start.4
  12.4 0.7 copy-start.1
Sparse Core Ops, SparseCore 0:
  59.2 37.8 reduce-scatter.1
